TPU v7x, 32 devices: a whole 2x2x4 slice. The times are simulated.
32 devices in a mesh: gx: 2 (over x), gy: 4 (over y, core), gz: 4 (over z).
Axes of the slice: x: 2, y: 2, z: 4, core: 2. Of those that a mesh axis runs over, the one named last changes fastest.
Arguments:
- field: float32 [448, 448, 448], P(('gx', 'gy'), 'gz'), may hold values from -6 to 6
- forward: float32 [2, 224, 224], replicated, may hold values from -0.375 to 0.375
- inverse: float32 [2, 224, 224], replicated, may hold values from -0.375 to 0.375
- eigen: float32 [448], replicated, may hold values from 0.05 to 20
Outputs:
- solution: float32 [448, 448, 448], P(('gx', 'gy'), 'gz')
All inputs are finite; a program needn't handle non-finite values.
Results may differ from a plain program's by a relative error of at most 0.000071.
Values sent between devices are 32-bit elements; how exact they have to be, the bound alone decides.
No kernel may reach another device: no remote copies, remote signals or barrier semaphores. Data moves between devices by JAX's collectives and lax.ppermute only.
A program may use at most 128 MiB of HBM per device.

v0:
```python
import math

import jax
import jax.numpy as jnp
from jax import lax
from jax.experimental import pallas as pl
from jax.experimental.pallas import tpu as pltpu
from jax.sharding import Mesh, PartitionSpec as P


AXES = ("xl", "gy", "zl")
LANES = 128
CHUNKS = ((16, 0), (24, None), (16, 1))


def split(x):
    high = x.astype(jnp.bfloat16)
    low = (x - high.astype(jnp.float32)).astype(jnp.bfloat16)
    return high, low


def dot3(a, b, dims):
    ah, al = a
    bh, bl = b
    dot = lambda u, v: lax.dot_general(u, v, (dims, ((), ())), preferred_element_type=jnp.float32)
    return dot(ah, bh) + (dot(ah, bl) + dot(al, bh))


def cut(total, parts):
    sizes = []
    for left in range(parts, 0, -1):
        sizes.append(-(-(total - sum(sizes)) // left))
    return sizes


def sending_order(count):
    far = [d for d in range(2, count) if 2 * d >= count]
    near = [d for d in range(1, count) if d not in far]
    order = [0]
    for pair in zip([d for d in far if d % 2 == 0], [d for d in near if d % 2 == 1]):
        order += pair
    return order + [d for d in far + near if d not in order]


def shares(count, chunk):
    return [count // 2 if chunk[1] is None else count * (chunk[1] == p) for p in range(2)]


def swap_blocks(x, index, axis):
    count = x.shape[axis]
    bits = count.bit_length() - 1
    shape = x.shape
    x = x.reshape(shape[:axis] + (2,) * bits + shape[axis + 1:])
    for bit in range(bits):
        at = axis + bits - 1 - bit
        x = jnp.where((index >> bit) & 1 == 1, jnp.flip(x, at), x)
    return x.reshape(shape)


def pad_last(x, axis, to):
    widths = [(0, 0)] * x.ndim
    widths[axis] = (0, to - x.shape[axis])
    return jnp.pad(x, widths)


def load_field(field_ref, data, sems, start, block):
    step = pl.program_id(0)
    copies = data.shape[0] // block

    def copy(r):
        source = field_ref.at[pl.ds((start + r) * block, block), pl.ds(0, data.shape[1])]
        return pltpu.make_async_copy(source, data.at[pl.ds(r * block, block), :], sems.at[r])

    @pl.when(step == 0)
    def _():
        for r in range(copies):
            copy(r).start()

    copy(step).wait()
    return data[pl.ds(pl.multiple_of(step * block, 8), block), :]


def write_pieces(result, out_refs):
    rows = out_refs[0].shape[0]
    for d, out in zip(sending_order(len(out_refs)), out_refs):
        out[...] = result[d * rows:(d + 1) * rows]


def lead_kernel(count, start, block, me_ref, forward_ref, field_ref, _, *refs):
    outs, (data, sems, matrix, weight_sem) = refs[:count], refs[count:]
    half = forward_ref.shape[2]
    rows = outs[0].shape[0]
    get = pltpu.make_async_copy(forward_ref.at[0], matrix, weight_sem)

    @pl.when(pl.program_id(0) == 0)
    def _():
        get.start()

    values = load_field(field_ref, data, sems, start, block)[:, :half]

    @pl.when(pl.program_id(0) == 0)
    def _():
        get.wait()

    weight = jnp.concatenate([matrix[pl.ds(pl.multiple_of((me_ref[0] ^ d) * rows, 8), rows), :] for d in range(count)], axis=0)
    write_pieces(dot3(split(weight), split(values), ((1,), (1,))), outs)


def next_kernel(count, start, block, weight_ref, field_ref, _, *refs):
    outs, (data, sems) = refs[:count], refs[count:]
    values = load_field(field_ref, data, sems, start, block)
    write_pieces(dot3(split(weight_ref[...]), split(values), ((1,), (1,))), outs)


def first_step(kernel, operands, specs, scratch, field, after, rows, count, start, number, width, block):
    hbm = pl.BlockSpec(memory_space=pl.ANY)
    return pl.pallas_call(
        lambda *refs: kernel(count, start, block, *refs),
        grid=(number,),
        in_specs=[*specs, hbm, hbm],
        out_specs=[pl.BlockSpec((rows, block), lambda r: (0, r))] * count,
        out_shape=[jax.ShapeDtypeStruct((rows, number * block), jnp.float32)] * count,
        scratch_shapes=[pltpu.VMEM((number * block, width), jnp.float32), pltpu.SemaphoreType.DMA((number,)), *scratch],
        cost_estimate=pl.CostEstimate(flops=6 * number * block * width * rows * count, bytes_accessed=4 * number * block * (width + rows * count), transcendentals=0),
    )(*operands, field, after)


def middle_kernel(i_local, k_local, count, units_in, units, eig_ref, ek_ref, ei_ref, fk_ref, fi_ref, gi_ref, gk_ref, *refs):
    given = count * len(units_in)
    ins, outs, work = refs[:given], refs[given:-2], refs[-2:]
    rows = ins[0].shape[0]
    place = [sending_order(count).index(d) for d in range(count)]
    i_blocks = count // 2
    period = math.lcm(k_local, LANES)
    i_per, tiles = period // k_local, period // LANES
    lane = lax.broadcasted_iota(jnp.int32, (rows, LANES), 1)

    for dy in range(i_blocks):
        begin = 0
        for s, number in enumerate(units_in):
            def spread(g, _, dy=dy, s=s, begin=begin):
                base = pl.multiple_of(g * period, LANES)
                for half in range(2):
                    ref = ins[s * count + place[2 * dy + half]]
                    data = [ref[:, pl.ds(base + LANES * q, LANES)] for q in range(tiles)]
                    for t in range(i_per):
                        q, off = divmod(t * k_local, LANES)
                        x = data[q]
                        if off + k_local > LANES:
                            x = jnp.where(lane >= off, x, data[q + 1])
                        if off:
                            x = pltpu.roll(x, LANES - off, 1)
                        at = pl.multiple_of((dy * i_local + (begin + g) * i_per + t) * rows, 8)
                        work[half][pl.ds(at, rows), :] = x
                return 0

            lax.fori_loop(0, number, spread, 0)
            begin += number

    fk, fi, gi, gk = split(fk_ref[...]), split(fi_ref[...]), split(gi_ref[...]), split(gk_ref[...])
    size = i_blocks * i_local
    eigen_ik = ei_ref[...] + ek_ref[...]

    def solve(j, _):
        x = jnp.concatenate([ref[pl.ds(j, size, stride=rows), :] for ref in work], axis=1)
        x = dot3(split(x), fk, ((1,), (0,)))
        x = dot3(fi, split(x), ((1,), (0,)))
        x = x / (eigen_ik + eig_ref[0, j])
        x = dot3(gi, split(x), ((1,), (0,)))
        x = dot3(split(x), gk, ((1,), (0,)))
        for half, ref in enumerate(work):
            ref[pl.ds(j, size, stride=rows), :] = x[:, half * LANES:(half + 1) * LANES]
        return 0

    lax.fori_loop(0, rows, solve, 0)

    for dy in range(i_blocks):
        begin = 0
        for s, number in enumerate(units):
            def gather(g, _, dy=dy, s=s, begin=begin):
                base = pl.multiple_of(g * period, LANES)
                for half in range(2):
                    data = []
                    for t in range(i_per):
                        at = pl.multiple_of((dy * i_local + (begin + g) * i_per + t) * rows, 8)
                        data.append(work[half][pl.ds(at, rows), :])
                    for q in range(tiles):
                        t, off = divmod(q * LANES, k_local)
                        left = k_local - off
                        x = pltpu.roll(data[t], LANES - off, 1) if off else data[t]
                        if left < LANES:
                            x = jnp.where(lane < left, x, pltpu.roll(data[t + 1], left, 1))
                        outs[s * count + place[2 * dy + half]][:, pl.ds(base + LANES * q, LANES)] = x
                return 0

            lax.fori_loop(0, number, gather, 0)
            begin += number


def middle_step(sent, eig, ek, ei, fk, fi, gi, gk, i_local, k_local, units_in, units):
    count = len(sent[0])
    rows = sent[0][0].shape[0]
    cells = i_local * k_local
    size = count // 2 * i_local
    vmem = pl.BlockSpec(memory_space=pltpu.VMEM)
    unit = cells // sum(units)
    pieces = [piece for part in sent for piece in part]
    outs = pl.pallas_call(
        lambda *refs: middle_kernel(i_local, k_local, count, units_in, units, *refs),
        in_specs=[pl.BlockSpec(memory_space=pltpu.SMEM)] + [vmem] * (6 + len(pieces)),
        out_specs=[vmem] * (count * len(units)),
        out_shape=[jax.ShapeDtypeStruct((rows, n * unit), jnp.float32) for n in units for _ in range(count)],
        scratch_shapes=[pltpu.VMEM((size * rows, LANES), jnp.float32)] * 2,
        cost_estimate=pl.CostEstimate(flops=4 * 6 * rows * size * 256 * 256, bytes_accessed=8 * rows * cells * count, transcendentals=0),
        name="middle",
    )(eig, ek, ei, fk, fi, gi, gk, *pieces)
    return [outs[s * count:(s + 1) * count] for s in range(len(units))]


def last_kernel(count, start, blocks, upper_ref, weight_ref, *refs):
    total = count * len(CHUNKS)
    pieces = refs[-6 - total:-6]
    out_ref, stage, result, matrix, in_sems, out_sems = refs[-6:]
    half = weight_ref.shape[2]
    get = pltpu.make_async_copy(weight_ref, matrix, out_sems.at[len(blocks)])
    get.start()

    def copies(b, at, size):
        found, row = [], 0
        for n, piece in enumerate(pieces):
            rows = piece.shape[0]
            base = start if n < total - count else 0
            to = row + sending_order(count)[n % count] * rows
            found.append(pltpu.make_async_copy(piece.at[:, pl.ds(base + at, size)], stage.at[pl.ds(to, rows), pl.ds(at, size)], in_sems.at[b, n]))
            if n % count == count - 1:
                row += count * rows
        return found

    def put(b, at, size):
        return pltpu.make_async_copy(result.at[pl.ds(at, size), :], out_ref.at[pl.ds(start + at, size), :], out_sems.at[b])

    spans = [(b, sum(blocks[:b]), size) for b, size in enumerate(blocks)]
    for span in spans:
        for copy in copies(*span):
            copy.start()
    get.wait()
    weights = [split(matrix[p]) for p in range(2)]
    for b, at, size in spans:
        for copy in copies(b, at, size):
            copy.wait()
        for p in range(2):
            parts, row = [], 0
            for chunk in CHUNKS:
                rows = shares(count, chunk)[p] * chunk[0]
                if chunk[1] is None:
                    parts.append(stage[pl.ds(pl.multiple_of(row + (upper_ref[0] ^ p) * rows, 8), rows), at:at + size])
                elif rows:
                    parts.append(stage[row:row + rows, at:at + size])
                row += count * chunk[0]
            values = split(jnp.concatenate(parts, axis=0))
            result[at:at + size, p * half:(p + 1) * half] = dot3(values, weights[p], ((0,), (0,)))
        put(b, at, size).start()
    for span in spans:
        put(*span).wait()


def last_step(upper, weight, chunks, out, start, blocks, cells, width):
    pieces = [piece for chunk in chunks for piece in chunk]
    before = [] if out is None else [out]
    operands = [upper, weight, *before, *pieces]
    hbm = pl.BlockSpec(memory_space=pl.ANY)
    specs = [pl.BlockSpec(memory_space=pltpu.SMEM)] + [hbm] * (len(operands) - 1)
    aliases = {2: 0} if before else {}
    lanes = sum(blocks)
    return pl.pallas_call(
        lambda *refs: last_kernel(len(chunks[0]), start, blocks, *refs),
        in_specs=specs,
        out_specs=hbm,
        out_shape=jax.ShapeDtypeStruct((cells, width), jnp.float32),
        input_output_aliases=aliases,
        scratch_shapes=[
            pltpu.VMEM((sum(piece.shape[0] for piece in pieces), lanes), jnp.float32),
            pltpu.VMEM((lanes, width), jnp.float32),
            pltpu.VMEM(weight.shape, jnp.float32),
            pltpu.SemaphoreType.DMA((len(blocks), len(pieces))),
            pltpu.SemaphoreType.DMA((len(blocks) + 1,)),
        ],
        cost_estimate=pl.CostEstimate(flops=6 * lanes * weight.size, bytes_accessed=8 * lanes * width, transcendentals=0),
        name="last",
    )(*operands)


def block_rows(matrix, chunk, starts, count, me):
    half = matrix.shape[1]
    parts = []
    for p, share in enumerate(shares(count, chunk)):
        if share:
            rows = matrix[p, starts[p]:starts[p] + share * chunk[0]]
            parts.append(jnp.pad(rows, ((0, 0), (p * half, (1 - p) * half))))
    rows = jnp.concatenate(parts, axis=0).reshape(count, chunk[0], 2 * half)
    return swap_blocks(rows, me, 0).reshape(-1, 2 * half)


def parity_rows(matrix, starts, count, me):
    sides = []
    for p in range(2):
        parts = []
        for chunk, start in zip(CHUNKS, starts):
            share = shares(count, chunk)[p]
            if share:
                rows = matrix[p, start[p]:start[p] + share * chunk[0]].reshape(share, chunk[0], -1)
                parts.append(swap_blocks(rows, me % share, 0).reshape(share * chunk[0], -1))
        sides.append(jnp.concatenate(parts, axis=0))
    return jnp.stack(sides)


def fast_body(count, field, forward, inverse, eigen):
    half = forward.shape[1]
    i_local, k_local, width = field.shape
    cells = i_local * k_local
    i_blocks = count // 2
    px, pz = lax.axis_index("px"), lax.axis_index("pz")
    me = lax.axis_index(AXES)
    me_l, me_i, upper = me % 2, me // 2, me // (count // 2)
    flat = field.reshape(cells, width)
    block = math.lcm(k_local, LANES)
    total = cells // block

    starts, at = [], (0, 0)
    for chunk in CHUNKS:
        starts.append(at)
        at = tuple(a + n * chunk[0] for a, n in zip(at, shares(count, chunk)))

    order = sending_order(count)

    def exchange(pieces):
        moved = [pieces[0]]
        for d, piece in zip(order[1:], pieces[1:]):
            moved.append(lax.ppermute(piece, AXES, [(s, s ^ d) for s in range(count)]))
        return moved

    vmem, smem, hbm = (pl.BlockSpec(memory_space=space) for space in (pltpu.VMEM, pltpu.SMEM, pl.ANY))
    scratch = [pltpu.VMEM((half, half), jnp.float32), pltpu.SemaphoreType.DMA]
    lead_width = -(-half // LANES) * LANES
    cut_in = [[total // 2, total - total // 2]] + [[total]] * (len(CHUNKS) - 1)
    cut_out = [[total]] * (len(CHUNKS) - 1) + [cut(total, min(total, 3))]
    sent = [[]]
    after, start = flat, 0
    for number in cut_in[0]:
        pieces = first_step(lead_kernel, (me.reshape(1), forward), [smem, hbm], scratch, flat, after, CHUNKS[0][0], count, start, number, lead_width, block)
        sent[0].append(exchange(pieces))
        after = pieces[0]
        start += number
    forward, inverse, eigen, _ = lax.optimization_barrier((forward, inverse, eigen, after))
    for chunk, start in zip(CHUNKS[1:], starts[1:]):
        weight = block_rows(forward, chunk, start, count, me)
        pieces = first_step(next_kernel, (weight,), [vmem], [], flat, after, chunk[0], count, 0, total, width, block)
        sent.append([exchange(pieces)])
        after = pieces[0]

    eigen2 = eigen.reshape(2, half)
    inverse_t = inverse.transpose(0, 2, 1)
    fk = swap_blocks(forward[pz].T.reshape(2, k_local, half), me_l, 0)
    fk = pad_last(fk, 1, LANES).reshape(2 * LANES, 2, k_local)
    fk = pad_last(fk, 2, LANES).reshape(2 * LANES, 2 * LANES)
    gk = swap_blocks(inverse_t[pz].reshape(half, 2, k_local), me_l, 1)
    gk = pad_last(gk, 2, LANES).reshape(2, k_local, 2 * LANES)
    gk = pad_last(gk, 1, LANES).reshape(2 * LANES, 2 * LANES)
    fi = swap_blocks(forward[px].reshape(half, i_blocks, i_local), me_i, 1).reshape(half, half)
    gi = swap_blocks(inverse[px].reshape(i_blocks, i_local, half), me_i, 0).reshape(half, half)
    ek = jnp.pad(eigen2[pz].reshape(2, k_local), ((0, 0), (0, LANES - k_local)), constant_values=1.0).reshape(1, 2 * LANES)
    ei = eigen2[px].reshape(half, 1)

    back = []
    for chunk, start, parts, units_in, units in zip(CHUNKS, starts, sent, cut_in, cut_out):
        if chunk[1] is None:
            own = upper * half + jnp.where(upper == 1, start[1], start[0]) + me % (count // 2) * chunk[0]
        else:
            own = chunk[1] * half + start[chunk[1]] + me * chunk[0]
        eig = lax.dynamic_slice_in_dim(eigen, own, chunk[0]).reshape(1, -1)
        done = middle_step(parts, eig, ek, ei, fk, fi, gi, gk, i_local, k_local, units_in, units)
        back.append([exchange(part) for part in done])
    weight = parity_rows(inverse_t, starts, count, me)
    whole = [parts[0] for parts in back[:-1]]
    out, at = None, 0
    for tail, number in zip(back[-1], cut_out[-1]):
        blocks = [block] * number
        if at + number * block == cells:
            blocks[-1:] = [LANES * n for n in cut(block // LANES, 2)]
        out = last_step(upper.reshape(1), weight, [*whole, tail], out, at, blocks, cells, width)
        at += number * block
    return out.reshape(field.shape)


def plain_body(count_i, count_k, field, forward, inverse, eigen):
    half = forward.shape[1]
    i_local, k_local, width = field.shape
    count = count_i * count_k
    rows = width // count
    high = lax.Precision.HIGHEST
    px, pz = lax.axis_index("px"), lax.axis_index("pz")
    me = lax.axis_index(AXES)
    eigen2 = eigen.reshape(2, half)
    x = jnp.einsum("pjm,ikpm->pjik", forward, field.reshape(i_local, k_local, 2, half), precision=high)
    x = lax.all_to_all(x.reshape(count, rows, i_local, k_local), AXES, split_axis=0, concat_axis=0, tiled=True)
    x = x.reshape(count_i, count_k, rows, i_local, k_local).transpose(2, 0, 3, 1, 4).reshape(rows, half, half)
    x = jnp.einsum("nk,jik->jin", forward[pz], x, precision=high)
    x = jnp.einsum("ni,jik->jnk", forward[px], x, precision=high)
    eig = lax.dynamic_slice_in_dim(eigen, me * rows, rows)
    x = x / (eigen2[px][None, :, None] + eigen2[pz][None, None, :] + eig[:, None, None])
    x = jnp.einsum("ni,jik->jnk", inverse[px], x, precision=high)
    x = jnp.einsum("nk,jik->jin", inverse[pz], x, precision=high)
    x = x.reshape(rows, count_i, i_local, count_k, k_local).transpose(1, 3, 0, 2, 4).reshape(count, rows, i_local, k_local)
    x = lax.all_to_all(x, AXES, split_axis=0, concat_axis=0, tiled=True)
    x = jnp.einsum("pjm,pmik->ikpj", inverse, x.reshape(2, half, i_local, k_local), precision=high)
    return x.reshape(field.shape)


def solution(mesh):
    gx, gy, gz = (mesh.shape[name] for name in ("gx", "gy", "gz"))
    parts = Mesh(mesh.devices.reshape(2, gx // 2, gy, 2, gz // 2), ("px", "xl", "gy", "pz", "zl"))
    count_i, count_k = gx // 2 * gy, gz // 2

    fast_mesh = count_k == 2 and count_i & (count_i - 1) == 0

    def body(field, forward, inverse, eigen):
        i_local, k_local, width = field.shape
        fast = (
            fast_mesh
            and k_local <= LANES
            and width == count_i * count_k * sum(chunk[0] for chunk in CHUNKS)
            and i_local * k_local % math.lcm(k_local, LANES) == 0
            and i_local * k_local > math.lcm(k_local, LANES)
        )
        if fast:
            return fast_body(count_i * count_k, field, forward, inverse, eigen)
        return plain_body(count_i, count_k, field, forward, inverse, eigen)

    spec = P(("px", "xl", "gy"), ("pz", "zl"), None)
    return jax.shard_map(body, mesh=parts, in_specs=(spec, P(), P(), P()), out_specs=spec, check_vma=False)
```

profile of v0, /device:TPU:0, one launch (start us, length us, event | category | flops | bytes accessed | tf_op | source)
XLA Modules:
  0.0 358.1 jit_solution(17062135413865218008)
XLA Ops:
  0.0 4.3 %shard_map.46 = (f32[16,2688]{1,0:T(8,128)}, f32[16,2688]{1,0:T(8,128)}, f32[16,2688]{1,0:T(8,128)}, f32[16,2688]{1,0:T(8,128)}, f32[16,2688]{1,0:T(8,128)}, /*i...) custom-call(s32[1]{0:T(128)} %bitcast.1.refs_0_, f32[2,224,224]{2,1,0:T(8,128)} %refs_1_.3, ...), custom_call_target="tpu_custom_call" | custom-call | flops 528482304 | bytes 4128768 | tf_op jit(solution)/shard_map/pallas_call | solution.py:117
  4.3 3.1 collective-permute-start
  9.0 5.5 %shard_map.47 = (f32[16,3584]{1,0:T(8,128)}, f32[16,3584]{1,0:T(8,128)}, f32[16,3584]{1,0:T(8,128)}, f32[16,3584]{1,0:T(8,128)}, f32[16,3584]{1,0:T(8,128)}, /*i...) custom-call(s32[1]{0:T(128)} %bitcast.1.refs_0_, f32[2,224,224]{2,1,0:T(8,128)} %refs_1_.3, ...), custom_call_target="tpu_custom_call" | custom-call | flops 704643072 | bytes 5505024 | tf_op jit(solution)/shard_map/pallas_call | solution.py:117
  16.5 11.1 %shard_map.48 = (f32[24,6272]{1,0:T(8,128)}, f32[24,6272]{1,0:T(8,128)}, f32[24,6272]{1,0:T(8,128)}, f32[24,6272]{1,0:T(8,128)}, f32[24,6272]{1,0:T(8,128)}, /*i...) custom-call(f32[192,448]{1,0:T(8,128)} %bitcast.59, f32[6272,448]{1,0:T(8,128)} %bitcast.55, ...), custom_call_target="tpu_custom_call" | custom-call | flops 3236954112 | bytes 16056320 | tf_op jit(solution)/shard_map/pallas_call | solution.py:117
  27.6 10.7 %shard_map.49 = (f32[16,6272]{1,0:T(8,128)}, f32[16,6272]{1,0:T(8,128)}, f32[16,6272]{1,0:T(8,128)}, f32[16,6272]{1,0:T(8,128)}, f32[16,6272]{1,0:T(8,128)}, /*i...) custom-call(f32[128,448]{1,0:T(8,128)} %bitcast.61, f32[6272,448]{1,0:T(8,128)} %bitcast.56, ...), custom_call_target="tpu_custom_call" | custom-call | flops 2157969408 | bytes 14450688 | tf_op jit(solution)/shard_map/pallas_call | solution.py:117
  44.7 10.5 %collective-permute-done.3.refs_11_ = f32[16,2688]{1,0:T(8,128)S(1)} collective-permute-done((f32[16,2688]{1,0:T(8,128)}, f32[16,2688]{1,0:T(8,128)S(1)}, u32[]{:S(2)}, u32[]{:S(2)}) %collective-permute-start.3) | collective-permute-done | bytes 172064 | tf_op jit(solution)/shard_map/ppermute | solution.py:339
  55.4 4.2 %collective-permute-done.4.refs_12_ = f32[16,2688]{1,0:T(8,128)S(1)} collective-permute-done((f32[16,2688]{1,0:T(8,128)}, f32[16,2688]{1,0:T(8,128)S(1)}, u32[]{:S(2)}, u32[]{:S(2)}) %collective-permute-start.4) | collective-permute-done | bytes 172064 | tf_op jit(solution)/shard_map/ppermute | solution.py:339
  69.8 7.1 %collective-permute-done.39.refs_12_ = f32[16,6272]{1,0:T(8,128)} collective-permute-done((f32[16,6272]{1,0:T(8,128)}, f32[16,6272]{1,0:T(8,128)}, u32[]{:S(2)}, u32[]{:S(2)}) %collective-permute-start.39) | collective-permute-done | bytes 401440 | tf_op jit(solution)/shard_map/ppermute | solution.py:339
  77.8 6.5 %collective-permute-done.40.refs_13_ = f32[16,6272]{1,0:T(8,128)} collective-permute-done((f32[16,6272]{1,0:T(8,128)}, f32[16,6272]{1,0:T(8,128)}, u32[]{:S(2)}, u32[]{:S(2)}) %collective-permute-start.40) | collective-permute-done | bytes 401440 | tf_op jit(solution)/shard_map/ppermute | solution.py:339
  86.3 30.0 %middle.5 = (f32[16,2688]{1,0:T(8,128)}, f32[16,2688]{1,0:T(8,128)}, f32[16,2688]{1,0:T(8,128)}, f32[16,2688]{1,0:T(8,128)}, f32[16,2688]{1,0:T(8,128)}, /*index...) custom-call(f32[1,16]{1,0:T(1,128)} %get-tuple-element.163.refs_0_, ...), custom_call_target="tpu_custom_call" | custom-call | flops 5637144576 | bytes 6422528 | tf_op jit(solution)/shard_map/middle/pallas_call | solution.py:208
  122.2 2.4 collective-permute-done.10.refs_19_
  125.1 5.0 %collective-permute-done.11.refs_20_ = f32[16,3584]{1,0:T(8,128)S(1)} collective-permute-done((f32[16,3584]{1,0:T(8,128)S(1)}, f32[16,3584]{1,0:T(8,128)S(1)}, u32[]{:S(2)}, u32[]{:S(2)}) %collective-permute-start.11) | collective-permute-done | bytes 229408 | tf_op jit(solution)/shard_map/ppermute | solution.py:339
  130.1 4.3 %collective-permute-done.12.refs_21_ = f32[16,3584]{1,0:T(8,128)S(1)} collective-permute-done((f32[16,3584]{1,0:T(8,128)S(1)}, f32[16,3584]{1,0:T(8,128)S(1)}, u32[]{:S(2)}, u32[]{:S(2)}) %collective-permute-start.12) | collective-permute-done | bytes 229408 | tf_op jit(solution)/shard_map/ppermute | solution.py:339
  135.5 2.1 collective-permute-start.53
  140.8 3.6 collective-permute-done.53.refs_24_
  145.9 2.7 collective-permute-start.42
  148.7 12.7 %collective-permute-done.56.refs_20_ = f32[16,1792]{1,0:T(8,128)S(1)} collective-permute-done((f32[16,1792]{1,0:T(8,128)}, f32[16,1792]{1,0:T(8,128)S(1)}, u32[]{:S(2)}, u32[]{:S(2)}) %collective-permute-start.56) | collective-permute-done | bytes 114720 | tf_op jit(solution)/shard_map/ppermute | solution.py:339
  165.0 2.9 collective-permute-done.43.refs_20_
  172.0 4.4 %collective-permute-done.46.refs_23_ = f32[16,2688]{1,0:T(8,128)S(1)} collective-permute-done((f32[16,2688]{1,0:T(8,128)}, f32[16,2688]{1,0:T(8,128)S(1)}, u32[]{:S(2)}, u32[]{:S(2)}) %collective-permute-start.46) | collective-permute-done | bytes 172064 | tf_op jit(solution)/shard_map/ppermute | solution.py:339
  182.0 30.2 %middle.3 = (f32[16,6272]{1,0:T(8,128)}, f32[16,6272]{1,0:T(8,128)}, f32[16,6272]{1,0:T(8,128)}, f32[16,6272]{1,0:T(8,128)}, f32[16,6272]{1,0:T(8,128)}, /*index...) custom-call(f32[1,16]{1,0:T(1,128)} %get-tuple-element.164.refs_0_, f32[1,256]{1,0:T(1,128)} %bitcast.84, ...), custom_call_target="tpu_custom_call" | custom-call | flops 5637144576 | bytes 6422528 | tf_op jit(solution)/shard_map/middle/pallas_call | solution.py:208
  212.1 2.3 collective-permute-start.14
  215.7 3.2 collective-permute-done.26.refs_13_
  220.0 39.1 %middle.4 = (f32[24,6272]{1,0:T(8,128)}, f32[24,6272]{1,0:T(8,128)}, f32[24,6272]{1,0:T(8,128)}, f32[24,6272]{1,0:T(8,128)}, f32[24,6272]{1,0:T(8,128)}, /*index...) custom-call(f32[1,24]{1,0:T(1,128)} %dynamic-slice_bitcast_fusion.1.refs_0_, f32[1,256]{1,0:T(1,128)} %bitcast.85, ...), custom_call_target="tpu_custom_call" | custom-call | flops 8455716864 | bytes 9633792 | tf_op jit(solution)/shard_map/middle/pallas_call | solution.py:208
  265.9 20.7 %collective-permute-done.18.refs_7_.refs_8_ = f32[16,6272]{1,0:T(8,128)S(1)} collective-permute-done((f32[16,6272]{1,0:T(8,128)}, f32[16,6272]{1,0:T(8,128)S(1)}, u32[]{:S(2)}, u32[]{:S(2)}) %collective-permute-start.18) | collective-permute-done | bytes 401440 | tf_op jit(solution)/shard_map/ppermute | solution.py:339
  286.6 6.2 %collective-permute-done.19.refs_8_.refs_9_ = f32[16,6272]{1,0:T(8,128)S(1)} collective-permute-done((f32[16,6272]{1,0:T(8,128)}, f32[16,6272]{1,0:T(8,128)S(1)}, u32[]{:S(2)}, u32[]{:S(2)}) %collective-permute-start.19) | collective-permute-done | bytes 401440 | tf_op jit(solution)/shard_map/ppermute | solution.py:339
  299.6 7.2 %collective-permute-done.30.refs_13_.refs_14_ = f32[24,6272]{1,0:T(8,128)S(1)} collective-permute-done((f32[24,6272]{1,0:T(8,128)}, f32[24,6272]{1,0:T(8,128)S(1)}, u32[]{:S(2)}, u32[]{:S(2)}) %collective-permute-start.30) | collective-permute-done | bytes 602144 | tf_op jit(solution)/shard_map/ppermute | solution.py:339
  310.9 12.9 %collective-permute-done.32.refs_15_.refs_16_ = f32[24,6272]{1,0:T(8,128)S(1)} collective-permute-done((f32[24,6272]{1,0:T(8,128)}, f32[24,6272]{1,0:T(8,128)S(1)}, u32[]{:S(2)}, u32[]{:S(2)}) %collective-permute-start.32) | collective-permute-done | bytes 602144 | tf_op jit(solution)/shard_map/ppermute | solution.py:339
  325.1 9.6 %collective-permute-done.33.refs_16_.refs_17_ = f32[24,6272]{1,0:T(8,128)} collective-permute-done((f32[24,6272]{1,0:T(8,128)}, f32[24,6272]{1,0:T(8,128)}, u32[]{:S(2)}, u32[]{:S(2)}) %collective-permute-start.33) | collective-permute-done | bytes 602144 | tf_op jit(solution)/shard_map/ppermute | solution.py:339
  334.7 2.8 collective-permute-start.61
  337.6 7.7 %last.3.refs_2_ = f32[6272,448]{1,0:T(8,128)} custom-call(s32[1]{0:T(128)} %bitcast.refs_0_, f32[2,224,224]{2,1,0:T(8,128)} %pad_maximum_fusion.refs_1_, f32[16,6272]{1,0:T(8,128)} %get-tuple-element.99.refs_2_.refs_3_, f32[16,6272]{1,0:T(8,128)} %copy-done.6, f32[16,6272]{1,0:T(8,128)} %copy-done.7, f32[16,6272]{1,0:T(8,128)} %copy-done.8, ...), custom_call_target="tpu_custom_call" | custom-call | flops 1618477056 | bytes 9633792 | tf_op jit(solution)/shard_map/last/pallas_call | solution.py:275
  345.2 5.9 %last.4.refs_2_ = f32[6272,448]{1,0:T(8,128)} custom-call(s32[1]{0:T(128)} %bitcast.refs_0_, f32[2,224,224]{2,1,0:T(8,128)} %pad_maximum_fusion.refs_1_, f32[6272,448]{1,0:T(8,128)} %last.3.refs_2_, f32[16,6272]{1,0:T(8,128)} %get-tuple-element.99.refs_2_.refs_3_, f32[16,6272]{1,0:T(8,128)} %copy-done.6, ...), custom_call_target="tpu_custom_call", output_to_operand_aliasing={{}: (2, {})} | custom-call | flops 1078984704 | bytes 6422528 | tf_op jit(solution)/shard_map/last/pallas_call | solution.py:275
  351.8 6.1 %last.5 = f32[6272,448]{1,0:T(8,128)} custom-call(s32[1]{0:T(128)} %bitcast.refs_0_, f32[2,224,224]{2,1,0:T(8,128)} %pad_maximum_fusion.refs_1_, f32[6272,448]{1,0:T(8,128)} %last.4.refs_2_, f32[16,6272]{1,0:T(8,128)} %get-tuple-element.99.refs_2_.refs_3_, f32[16,6272]{1,0:T(8,128)} %copy-done.6, ...), custom_call_target="tpu_custom_call", output_to_operand_aliasing={{}: (2, {})} | custom-call | flops 1078984704 | bytes 6422528 | tf_op jit(solution)/shard_map/last/pallas_call | solution.py:275
  (259 shorter events, 70.3 us)
Async XLA Ops:
  4.3 36.0 %collective-permute-start = (f32[16,2688]{1,0:T(8,128)}, f32[16,2688]{1,0:T(8,128)S(1)}, u32[]{:S(2)}, u32[]{:S(2)}) collective-permute-start(f32[16,2688]{1,0:T(8,128)} %get-tuple-element.85), channel_id=1, source_target_pairs={{0,8},{1,9},{4,12},{5,13},{8,0},{9,1},{12,4},{13,5},{2,10},{3,11},... | collective-permute-start | bytes 516104 | tf_op jit(solution)/shard_map/ppermute | solution.py:339
  7.4 34.8 %collective-permute-start.1 = (f32[16,2688]{1,0:T(8,128)}, f32[16,2688]{1,0:T(8,128)S(1)}, u32[]{:S(2)}, u32[]{:S(2)}) collective-permute-start(f32[16,2688]{1,0:T(8,128)} %get-tuple-element.86), channel_id=1, source_target_pairs={{0,1},{1,0},{4,5},{5,4},{8,9},{9,8},{12,13},{13,12},{2,3},{3,2},{6... | collective-permute-start | bytes 516104 | tf_op jit(solution)/shard_map/ppermute | solution.py:339
  9.0 34.2 %collective-permute-start.2 = (f32[16,2688]{1,0:T(8,128)}, f32[16,2688]{1,0:T(8,128)S(1)}, u32[]{:S(2)}, u32[]{:S(2)}) collective-permute-start(f32[16,2688]{1,0:T(8,128)} %get-tuple-element.87), channel_id=1, source_target_pairs={{0,12},{1,13},{4,8},{5,9},{8,4},{9,5},{12,0},{13,1},{2,14},{3,15},... | collective-permute-start | bytes 516104 | tf_op jit(solution)/shard_map/ppermute | solution.py:339
  43.9 25.1 %collective-permute-start.37 = (f32[16,6272]{1,0:T(8,128)}, f32[16,6272]{1,0:T(8,128)S(1)}, u32[]{:S(2)}, u32[]{:S(2)}) collective-permute-start(f32[16,6272]{1,0:T(8,128)} %get-tuple-element.126), channel_id=1, source_target_pairs={{0,12},{1,13},{4,8},{5,9},{8,4},{9,5},{12,0},{13,1},{2,14},{3,15},... | collective-permute-start | bytes 1204232 | tf_op jit(solution)/shard_map/ppermute | solution.py:339
  68.9 47.4 %collective-permute-start.5 = (f32[16,2688]{1,0:T(8,128)}, f32[16,2688]{1,0:T(8,128)S(1)}, u32[]{:S(2)}, u32[]{:S(2)}) collective-permute-start(f32[16,2688]{1,0:T(8,128)} %get-tuple-element.90), channel_id=1, source_target_pairs={{0,13},{1,12},{4,9},{5,8},{8,5},{9,4},{12,1},{13,0},{2,15},{3,14},... | collective-permute-start | bytes 516104 | tf_op jit(solution)/shard_map/ppermute | solution.py:339
  69.3 48.9 %collective-permute-start.6 = (f32[16,2688]{1,0:T(8,128)}, f32[16,2688]{1,0:T(8,128)}, u32[]{:S(2)}, u32[]{:S(2)}) collective-permute-start(f32[16,2688]{1,0:T(8,128)} %get-tuple-element.91), channel_id=1, source_target_pairs={{0,4},{1,5},{4,0},{5,1},{8,12},{9,13},{12,8},{13,9},{2,6},{3,7},{6... | collective-permute-start | bytes 516104 | tf_op jit(solution)/shard_map/ppermute | solution.py:339
  76.9 41.6 %collective-permute-start.7 = (f32[16,3584]{1,0:T(8,128)}, f32[16,3584]{1,0:T(8,128)S(1)}, u32[]{:S(2)}, u32[]{:S(2)}) collective-permute-start(f32[16,3584]{1,0:T(8,128)} %get-tuple-element.92), channel_id=1, source_target_pairs={{0,8},{1,9},{4,12},{5,13},{8,0},{9,1},{12,4},{13,5},{2,10},{3,11},... | collective-permute-start | bytes 688136 | tf_op jit(solution)/shard_map/ppermute | solution.py:339
  84.3 36.1 %collective-permute-start.8 = (f32[16,3584]{1,0:T(8,128)}, f32[16,3584]{1,0:T(8,128)S(1)}, u32[]{:S(2)}, u32[]{:S(2)}) collective-permute-start(f32[16,3584]{1,0:T(8,128)} %get-tuple-element.93), channel_id=1, source_target_pairs={{0,1},{1,0},{4,5},{5,4},{8,9},{9,8},{12,13},{13,12},{2,3},{3,2},{6... | collective-permute-start | bytes 688136 | tf_op jit(solution)/shard_map/ppermute | solution.py:339
  84.7 36.8 %collective-permute-start.9 = (f32[16,3584]{1,0:T(8,128)}, f32[16,3584]{1,0:T(8,128)S(1)}, u32[]{:S(2)}, u32[]{:S(2)}) collective-permute-start(f32[16,3584]{1,0:T(8,128)} %get-tuple-element.94), channel_id=1, source_target_pairs={{0,12},{1,13},{4,8},{5,9},{8,4},{9,5},{12,0},{13,1},{2,14},{3,15},... | collective-permute-start | bytes 688136 | tf_op jit(solution)/shard_map/ppermute | solution.py:339
  138.9 40.4 %collective-permute-start.21 = (f32[24,6272]{1,0:T(8,128)}, f32[24,6272]{1,0:T(8,128)}, u32[]{:S(2)}, u32[]{:S(2)}) collective-permute-start(f32[24,6272]{1,0:T(8,128)} %get-tuple-element.108), channel_id=1, source_target_pairs={{0,8},{1,9},{4,12},{5,13},{8,0},{9,1},{12,4},{13,5},{2,10},{3,11},... | collective-permute-start | bytes 1806344 | tf_op jit(solution)/shard_map/ppermute | solution.py:339
  139.2 42.1 %collective-permute-start.22 = (f32[24,6272]{1,0:T(8,128)}, f32[24,6272]{1,0:T(8,128)}, u32[]{:S(2)}, u32[]{:S(2)}) collective-permute-start(f32[24,6272]{1,0:T(8,128)} %get-tuple-element.109), channel_id=1, source_target_pairs={{0,1},{1,0},{4,5},{5,4},{8,9},{9,8},{12,13},{13,12},{2,3},{3,2},{6... | collective-permute-start | bytes 1806344 | tf_op jit(solution)/shard_map/ppermute | solution.py:339
  171.7 40.4 %collective-permute-start.23 = (f32[24,6272]{1,0:T(8,128)}, f32[24,6272]{1,0:T(8,128)}, u32[]{:S(2)}, u32[]{:S(2)}) collective-permute-start(f32[24,6272]{1,0:T(8,128)} %get-tuple-element.110), channel_id=1, source_target_pairs={{0,12},{1,13},{4,8},{5,9},{8,4},{9,5},{12,0},{13,1},{2,14},{3,15},... | collective-permute-start | bytes 1806344 | tf_op jit(solution)/shard_map/ppermute | solution.py:339
  176.4 38.1 %collective-permute-start.24 = (f32[24,6272]{1,0:T(8,128)}, f32[24,6272]{1,0:T(8,128)}, u32[]{:S(2)}, u32[]{:S(2)}) collective-permute-start(f32[24,6272]{1,0:T(8,128)} %get-tuple-element.111), channel_id=1, source_target_pairs={{0,5},{1,4},{4,1},{5,0},{8,13},{9,12},{12,9},{13,8},{2,7},{3,6},{6... | collective-permute-start | bytes 1806344 | tf_op jit(solution)/shard_map/ppermute | solution.py:339
  178.4 36.3 %collective-permute-start.25 = (f32[24,6272]{1,0:T(8,128)}, f32[24,6272]{1,0:T(8,128)}, u32[]{:S(2)}, u32[]{:S(2)}) collective-permute-start(f32[24,6272]{1,0:T(8,128)} %get-tuple-element.112), channel_id=1, source_target_pairs={{0,9},{1,8},{4,13},{5,12},{8,1},{9,0},{12,5},{13,4},{2,11},{3,10},... | collective-permute-start | bytes 1806344 | tf_op jit(solution)/shard_map/ppermute | solution.py:339
  179.2 39.6 %collective-permute-start.26 = (f32[24,6272]{1,0:T(8,128)}, f32[24,6272]{1,0:T(8,128)}, u32[]{:S(2)}, u32[]{:S(2)}) collective-permute-start(f32[24,6272]{1,0:T(8,128)} %get-tuple-element.113), channel_id=1, source_target_pairs={{0,13},{1,12},{4,9},{5,8},{8,5},{9,4},{12,1},{13,0},{2,15},{3,14},... | collective-permute-start | bytes 1806344 | tf_op jit(solution)/shard_map/ppermute | solution.py:339
  181.3 37.9 %collective-permute-start.27 = (f32[24,6272]{1,0:T(8,128)}, f32[24,6272]{1,0:T(8,128)}, u32[]{:S(2)}, u32[]{:S(2)}) collective-permute-start(f32[24,6272]{1,0:T(8,128)} %get-tuple-element.114), channel_id=1, source_target_pairs={{0,4},{1,5},{4,0},{5,1},{8,12},{9,13},{12,8},{13,9},{2,6},{3,7},{6... | collective-permute-start | bytes 1806344 | tf_op jit(solution)/shard_map/ppermute | solution.py:339
  212.1 48.9 %collective-permute-start.14 = (f32[16,6272]{1,0:T(8,128)}, f32[16,6272]{1,0:T(8,128)S(1)}, u32[]{:S(2)}, u32[]{:S(2)}) collective-permute-start(f32[16,6272]{1,0:T(8,128)} %get-tuple-element.100), channel_id=1, source_target_pairs={{0,8},{1,9},{4,12},{5,13},{8,0},{9,1},{12,4},{13,5},{2,10},{3,11},... | collective-permute-start | bytes 1204232 | tf_op jit(solution)/shard_map/ppermute | solution.py:339
  214.5 47.3 %collective-permute-start.15 = (f32[16,6272]{1,0:T(8,128)}, f32[16,6272]{1,0:T(8,128)S(1)}, u32[]{:S(2)}, u32[]{:S(2)}) collective-permute-start(f32[16,6272]{1,0:T(8,128)} %get-tuple-element.101), channel_id=1, source_target_pairs={{0,1},{1,0},{4,5},{5,4},{8,9},{9,8},{12,13},{13,12},{2,3},{3,2},{6... | collective-permute-start | bytes 1204232 | tf_op jit(solution)/shard_map/ppermute | solution.py:339
  214.7 48.7 %collective-permute-start.16 = (f32[16,6272]{1,0:T(8,128)}, f32[16,6272]{1,0:T(8,128)S(1)}, u32[]{:S(2)}, u32[]{:S(2)}) collective-permute-start(f32[16,6272]{1,0:T(8,128)} %get-tuple-element.102), channel_id=1, source_target_pairs={{0,12},{1,13},{4,8},{5,9},{8,4},{9,5},{12,0},{13,1},{2,14},{3,15},... | collective-permute-start | bytes 1204232 | tf_op jit(solution)/shard_map/ppermute | solution.py:339
  218.9 44.7 %collective-permute-start.17 = (f32[16,6272]{1,0:T(8,128)}, f32[16,6272]{1,0:T(8,128)S(1)}, u32[]{:S(2)}, u32[]{:S(2)}) collective-permute-start(f32[16,6272]{1,0:T(8,128)} %get-tuple-element.103), channel_id=1, source_target_pairs={{0,5},{1,4},{4,1},{5,0},{8,13},{9,12},{12,9},{13,8},{2,7},{3,6},{6... | collective-permute-start | bytes 1204232 | tf_op jit(solution)/shard_map/ppermute | solution.py:339
  219.2 40.0 %collective-permute-start.48 = (f32[16,2688]{1,0:T(8,128)S(1)}, f32[16,2688]{1,0:T(8,128)S(1)}, u32[]{:S(2)}, u32[]{:S(2)}) collective-permute-start(f32[16,2688]{1,0:T(8,128)S(1)} %copy-done.50), channel_id=1, source_target_pairs={{0,4},{1,5},{4,0},{5,1},{8,12},{9,13},{12,8},{13,9},{2,6},{3,7},{6... | collective-permute-start | bytes 516104 | tf_op jit(solution)/shard_map/ppermute | solution.py:339
  259.8 36.4 %collective-permute-start.28 = (f32[24,6272]{1,0:T(8,128)}, f32[24,6272]{1,0:T(8,128)S(1)}, u32[]{:S(2)}, u32[]{:S(2)}) collective-permute-start(f32[24,6272]{1,0:T(8,128)} %get-tuple-element.116), channel_id=1, source_target_pairs={{0,8},{1,9},{4,12},{5,13},{8,0},{9,1},{12,4},{13,5},{2,10},{3,11},... | collective-permute-start | bytes 1806344 | tf_op jit(solution)/shard_map/ppermute | solution.py:339
  261.1 35.3 %collective-permute-start.29 = (f32[24,6272]{1,0:T(8,128)}, f32[24,6272]{1,0:T(8,128)S(1)}, u32[]{:S(2)}, u32[]{:S(2)}) collective-permute-start(f32[24,6272]{1,0:T(8,128)} %get-tuple-element.117), channel_id=1, source_target_pairs={{0,1},{1,0},{4,5},{5,4},{8,9},{9,8},{12,13},{13,12},{2,3},{3,2},{6... | collective-permute-start | bytes 1806344 | tf_op jit(solution)/shard_map/ppermute | solution.py:339
  261.8 24.8 %collective-permute-start.18 = (f32[16,6272]{1,0:T(8,128)}, f32[16,6272]{1,0:T(8,128)S(1)}, u32[]{:S(2)}, u32[]{:S(2)}) collective-permute-start(f32[16,6272]{1,0:T(8,128)} %get-tuple-element.104), channel_id=1, source_target_pairs={{0,9},{1,8},{4,13},{5,12},{8,1},{9,0},{12,5},{13,4},{2,11},{3,10},... | collective-permute-start | bytes 1204232 | tf_op jit(solution)/shard_map/ppermute | solution.py:339
  263.4 29.4 %collective-permute-start.19 = (f32[16,6272]{1,0:T(8,128)}, f32[16,6272]{1,0:T(8,128)S(1)}, u32[]{:S(2)}, u32[]{:S(2)}) collective-permute-start(f32[16,6272]{1,0:T(8,128)} %get-tuple-element.105), channel_id=1, source_target_pairs={{0,13},{1,12},{4,9},{5,8},{8,5},{9,4},{12,1},{13,0},{2,15},{3,14},... | collective-permute-start | bytes 1204232 | tf_op jit(solution)/shard_map/ppermute | solution.py:339
  263.6 31.0 %collective-permute-start.20 = (f32[16,6272]{1,0:T(8,128)}, f32[16,6272]{1,0:T(8,128)S(1)}, u32[]{:S(2)}, u32[]{:S(2)}) collective-permute-start(f32[16,6272]{1,0:T(8,128)} %get-tuple-element.106), channel_id=1, source_target_pairs={{0,4},{1,5},{4,0},{5,1},{8,12},{9,13},{12,8},{13,9},{2,6},{3,7},{6... | collective-permute-start | bytes 1204232 | tf_op jit(solution)/shard_map/ppermute | solution.py:339
  294.6 29.3 %collective-permute-start.32 = (f32[24,6272]{1,0:T(8,128)}, f32[24,6272]{1,0:T(8,128)S(1)}, u32[]{:S(2)}, u32[]{:S(2)}) collective-permute-start(f32[24,6272]{1,0:T(8,128)} %get-tuple-element.120), channel_id=1, source_target_pairs={{0,9},{1,8},{4,13},{5,12},{8,1},{9,0},{12,5},{13,4},{2,11},{3,10},... | collective-permute-start | bytes 1806344 | tf_op jit(solution)/shard_map/ppermute | solution.py:339
  296.3 38.4 %collective-permute-start.33 = (f32[24,6272]{1,0:T(8,128)}, f32[24,6272]{1,0:T(8,128)}, u32[]{:S(2)}, u32[]{:S(2)}) collective-permute-start(f32[24,6272]{1,0:T(8,128)} %get-tuple-element.121), channel_id=1, source_target_pairs={{0,13},{1,12},{4,9},{5,8},{8,5},{9,4},{12,1},{13,0},{2,15},{3,14},... | collective-permute-start | bytes 1806344 | tf_op jit(solution)/shard_map/ppermute | solution.py:339
  296.3 41.2 %collective-permute-start.34 = (f32[24,6272]{1,0:T(8,128)}, f32[24,6272]{1,0:T(8,128)}, u32[]{:S(2)}, u32[]{:S(2)}) collective-permute-start(f32[24,6272]{1,0:T(8,128)} %get-tuple-element.122), channel_id=1, source_target_pairs={{0,4},{1,5},{4,0},{5,1},{8,12},{9,13},{12,8},{13,9},{2,6},{3,7},{6... | collective-permute-start | bytes 1806344 | tf_op jit(solution)/shard_map/ppermute | solution.py:339
  306.9 44.3 %collective-permute-start.58 = (f32[16,1792]{1,0:T(8,128)}, f32[16,1792]{1,0:T(8,128)S(1)}, u32[]{:S(2)}, u32[]{:S(2)}) collective-permute-start(f32[16,1792]{1,0:T(8,128)} %get-tuple-element.150), channel_id=1, source_target_pairs={{0,12},{1,13},{4,8},{5,9},{8,4},{9,5},{12,0},{13,1},{2,14},{3,15},... | collective-permute-start | bytes 344072 | tf_op jit(solution)/shard_map/ppermute | solution.py:339
  308.8 42.3 %collective-permute-start.59 = (f32[16,1792]{1,0:T(8,128)}, f32[16,1792]{1,0:T(8,128)}, u32[]{:S(2)}, u32[]{:S(2)}) collective-permute-start(f32[16,1792]{1,0:T(8,128)} %get-tuple-element.151), channel_id=1, source_target_pairs={{0,5},{1,4},{4,1},{5,0},{8,13},{9,12},{12,9},{13,8},{2,7},{3,6},{6... | collective-permute-start | bytes 344072 | tf_op jit(solution)/shard_map/ppermute | solution.py:339
  323.8 27.4 %collective-permute-start.60 = (f32[16,1792]{1,0:T(8,128)}, f32[16,1792]{1,0:T(8,128)}, u32[]{:S(2)}, u32[]{:S(2)}) collective-permute-start(f32[16,1792]{1,0:T(8,128)} %get-tuple-element.152), channel_id=1, source_target_pairs={{0,9},{1,8},{4,13},{5,12},{8,1},{9,0},{12,5},{13,4},{2,11},{3,10},... | collective-permute-start | bytes 344072 | tf_op jit(solution)/shard_map/ppermute | solution.py:339
  (83 other events, 2115.7 us)
where the time goes:
time: 358 us
  Pallas kernels  151 us (42%)
  waiting for transfers between devices  130 us (36%)
  starting transfers between devices  62.1 us (17%)
  local copies, waits for them, and re-layouts  8.78 us (2%)
  other arithmetic  6.1 us (2%)
    ppermute x63, waiting for transfers between devices, exchange(): moved.append(lax.ppermute(piece, AXES, [(s, s ^ d) for s in range(count)]))  130 us
    pallas_call x3, Pallas kernels, middle_step(): pl.pallas_call(lambda *refs: middle_kernel(i_local, k_local, count, units...  99.3 us
    ppermute x63, starting transfers between devices, exchange(): moved.append(lax.ppermute(piece, AXES, [(s, s ^ d) for s in range(count)]))  62.1 us
    pallas_call x4, Pallas kernels, first_step(): pl.pallas_call(lambda *refs: kernel(count, start, block, *refs), grid=(nu...  31.6 us
    pallas_call x3, Pallas kernels, last_step(): pl.pallas_call(lambda *refs: last_kernel(len(chunks[0]), start, blocks, *...  19.7 us
  transfers between devices with their start and end apart: 63, of which 23 were waited for; matrix products, arithmetic and copies ran while one was open for 4% of the time, Pallas kernels for 39%

commit v1 on v0

--- a/solution.py
+++ b/solution.py
@@ -10,7 +10,7 @@
 
 AXES = ("xl", "gy", "zl")
 LANES = 128
-CHUNKS = ((16, 0), (24, None), (16, 1))
+CHUNKS = ((24, 0), (8, None), (24, 1))
 
 
 def split(x):
@@ -343,7 +343,7 @@
     scratch = [pltpu.VMEM((half, half), jnp.float32), pltpu.SemaphoreType.DMA]
     lead_width = -(-half // LANES) * LANES
     cut_in = [[total // 2, total - total // 2]] + [[total]] * (len(CHUNKS) - 1)
-    cut_out = [[total]] * (len(CHUNKS) - 1) + [cut(total, min(total, 3))]
+    cut_out = [[total]] * (len(CHUNKS) - 1) + [[total - 3, 2, 1]]
     sent = [[]]
     after, start = flat, 0
     for number in cut_in[0]:
@@ -378,6 +378,8 @@
         else:
             own = chunk[1] * half + start[chunk[1]] + me * chunk[0]
         eig = lax.dynamic_slice_in_dim(eigen, own, chunk[0]).reshape(1, -1)
+        if back:
+            eig, _ = lax.optimization_barrier((eig, back[-1][0][0]))
         done = middle_step(parts, eig, ek, ei, fk, fi, gi, gk, i_local, k_local, units_in, units)
         back.append([exchange(part) for part in done])
     weight = parity_rows(inverse_t, starts, count, me)
@@ -430,7 +432,7 @@
             and k_local <= LANES
             and width == count_i * count_k * sum(chunk[0] for chunk in CHUNKS)
             and i_local * k_local % math.lcm(k_local, LANES) == 0
-            and i_local * k_local > math.lcm(k_local, LANES)
+            and i_local * k_local >= 4 * math.lcm(k_local, LANES)
         )
         if fast:
             return fast_body(count_i * count_k, field, forward, inverse, eigen)

time: 358 us -> 356 us (level)
  Pallas kernels: 151 us -> 146 us
    pallas_call x3, Pallas kernels: 99.3 us -> 95.5 us  [middle_step(): pl.pallas_call(lambda *refs: middle_kernel(i_local, k_local, count, units...]
  transfers between devices with their start and end apart: 63 -> 63, of which waited for: 23 -> 19; matrix products, arithmetic and copies ran while one was open for 4% -> 4% of each run, Pallas kernels for 39% -> 39%
where the time goes in v1:
time: 356 us; the launch traced here: 355 us
  Pallas kernels  146 us (41%)
  waiting for transfers between devices  132 us (37%)
  starting transfers between devices  60.2 us (17%)
  local copies, waits for them, and re-layouts  9.6 us (3%)
  other arithmetic  6.68 us (2%)
    ppermute x63, waiting for transfers between devices, exchange(): moved.append(lax.ppermute(piece, AXES, [(s, s ^ d) for s in range(count)]))  132 us
    pallas_call x3, Pallas kernels, middle_step(): pl.pallas_call(lambda *refs: middle_kernel(i_local, k_local, count, units...  95.5 us
    ppermute x63, starting transfers between devices, exchange(): moved.append(lax.ppermute(piece, AXES, [(s, s ^ d) for s in range(count)]))  60.2 us
    pallas_call x4, Pallas kernels, first_step(): pl.pallas_call(lambda *refs: kernel(count, start, block, *refs), grid=(nu...  31.4 us
    pallas_call x3, Pallas kernels, last_step(): pl.pallas_call(lambda *refs: last_kernel(len(chunks[0]), start, blocks, *...  19.6 us
  transfers between devices with their start and end apart: 63, of which 19 were waited for; matrix products, arithmetic and copies ran while one was open for 4% of the time, Pallas kernels for 39%

profile of v1, /device:TPU:0, one launch (start us, length us, event | category | flops | bytes accessed | tf_op | source)
XLA Modules:
  0.0 355.5 jit_solution(7030809287561931392)
XLA Ops:
  0.0 4.4 %shard_map.46 = (f32[24,2688]{1,0:T(8,128)}, f32[24,2688]{1,0:T(8,128)}, f32[24,2688]{1,0:T(8,128)}, f32[24,2688]{1,0:T(8,128)}, f32[24,2688]{1,0:T(8,128)}, /*i...) custom-call(s32[1]{0:T(128)} %bitcast.1.refs_0_, f32[2,224,224]{2,1,0:T(8,128)} %refs_1_.3, ...), custom_call_target="tpu_custom_call" | custom-call | flops 792723456 | bytes 4816896 | tf_op jit(solution)/shard_map/pallas_call | solution.py:117
  4.5 3.1 collective-permute-start
  9.1 5.6 %shard_map.47 = (f32[24,3584]{1,0:T(8,128)}, f32[24,3584]{1,0:T(8,128)}, f32[24,3584]{1,0:T(8,128)}, f32[24,3584]{1,0:T(8,128)}, f32[24,3584]{1,0:T(8,128)}, /*i...) custom-call(s32[1]{0:T(128)} %bitcast.1.refs_0_, f32[2,224,224]{2,1,0:T(8,128)} %refs_1_.3, ...), custom_call_target="tpu_custom_call" | custom-call | flops 1056964608 | bytes 6422528 | tf_op jit(solution)/shard_map/pallas_call | solution.py:117
  15.6 10.3 %shard_map.48 = (f32[8,6272]{1,0:T(8,128)}, f32[8,6272]{1,0:T(8,128)}, f32[8,6272]{1,0:T(8,128)}, f32[8,6272]{1,0:T(8,128)}, f32[8,6272]{1,0:T(8,128)}, /*index=...) custom-call(f32[64,448]{1,0:T(8,128)} %bitcast.71, f32[6272,448]{1,0:T(8,128)} %bitcast.55, ...), custom_call_target="tpu_custom_call" | custom-call | flops 1078984704 | bytes 12845056 | tf_op jit(solution)/shard_map/pallas_call | solution.py:117
  28.2 5.8 %collective-permute-done.21.refs_8_ = f32[8,6272]{1,0:T(8,128)S(1)} collective-permute-done((f32[8,6272]{1,0:T(8,128)}, f32[8,6272]{1,0:T(8,128)S(1)}, u32[]{:S(2)}, u32[]{:S(2)}) %collective-permute-start.21) | collective-permute-done | bytes 200736 | tf_op jit(solution)/shard_map/ppermute | solution.py:339
  36.6 10.2 %collective-permute-done.24.refs_11_ = f32[8,6272]{1,0:T(8,128)S(1)} collective-permute-done((f32[8,6272]{1,0:T(8,128)}, f32[8,6272]{1,0:T(8,128)S(1)}, u32[]{:S(2)}, u32[]{:S(2)}) %collective-permute-start.24) | collective-permute-done | bytes 200736 | tf_op jit(solution)/shard_map/ppermute | solution.py:339
  49.9 2.0 collective-permute-start.8
  53.4 3.9 %collective-permute-done.4.refs_12_ = f32[24,2688]{1,0:T(8,128)} collective-permute-done((f32[24,2688]{1,0:T(8,128)}, f32[24,2688]{1,0:T(8,128)}, u32[]{:S(2)}, u32[]{:S(2)}) %collective-permute-start.4) | collective-permute-done | bytes 258080 | tf_op jit(solution)/shard_map/ppermute | solution.py:339
  57.3 3.8 %collective-permute-done.5.refs_13_ = f32[24,2688]{1,0:T(8,128)} collective-permute-done((f32[24,2688]{1,0:T(8,128)}, f32[24,2688]{1,0:T(8,128)}, u32[]{:S(2)}, u32[]{:S(2)}) %collective-permute-start.5) | collective-permute-done | bytes 258080 | tf_op jit(solution)/shard_map/ppermute | solution.py:339
  63.5 5.7 %collective-permute-done.7.refs_16_ = f32[24,3584]{1,0:T(8,128)S(1)} collective-permute-done((f32[24,3584]{1,0:T(8,128)}, f32[24,3584]{1,0:T(8,128)S(1)}, u32[]{:S(2)}, u32[]{:S(2)}) %collective-permute-start.7) | collective-permute-done | bytes 344096 | tf_op jit(solution)/shard_map/ppermute | solution.py:339
  76.3 11.1 %shard_map.49 = (f32[24,6272]{1,0:T(8,128)}, f32[24,6272]{1,0:T(8,128)}, f32[24,6272]{1,0:T(8,128)}, f32[24,6272]{1,0:T(8,128)}, f32[24,6272]{1,0:T(8,128)}, /*i...) custom-call(f32[192,448]{1,0:T(8,128)} %bitcast.59, f32[6272,448]{1,0:T(8,128)} %bitcast.56, ...), custom_call_target="tpu_custom_call" | custom-call | flops 3236954112 | bytes 16056320 | tf_op jit(solution)/shard_map/pallas_call | solution.py:117
  92.6 39.2 %middle.3 = (f32[24,6272]{1,0:T(8,128)}, f32[24,6272]{1,0:T(8,128)}, f32[24,6272]{1,0:T(8,128)}, f32[24,6272]{1,0:T(8,128)}, f32[24,6272]{1,0:T(8,128)}, /*index...) custom-call(f32[1,24]{1,0:T(1,128)} %get-tuple-element.168.refs_0_, f32[1,256]{1,0:T(1,128)} %bitcast.83, ...), custom_call_target="tpu_custom_call" | custom-call | flops 8455716864 | bytes 9633792 | tf_op jit(solution)/shard_map/middle/pallas_call | solution.py:208
  133.6 17.0 %middle.4 = (f32[8,6272]{1,0:T(8,128)}, f32[8,6272]{1,0:T(8,128)}, f32[8,6272]{1,0:T(8,128)}, f32[8,6272]{1,0:T(8,128)}, f32[8,6272]{1,0:T(8,128)}, /*index=5*/f...) custom-call(f32[1,8]{1,0:T(1,128)} %dynamic-slice_bitcast_fusion.1.refs_0_, f32[1,256]{1,0:T(1,128)} %bitcast.84, ...), custom_call_target="tpu_custom_call" | custom-call | flops 2818572288 | bytes 3211264 | tf_op jit(solution)/shard_map/middle/pallas_call | solution.py:208
  151.6 6.5 %collective-permute-done.28.refs_11_.refs_12_ = f32[8,6272]{1,0:T(8,128)S(1)} collective-permute-done((f32[8,6272]{1,0:T(8,128)}, f32[8,6272]{1,0:T(8,128)S(1)}, u32[]{:S(2)}, u32[]{:S(2)}) %collective-permute-start.28) | collective-permute-done | bytes 200736 | tf_op jit(solution)/shard_map/ppermute | solution.py:339
  164.2 11.5 %collective-permute-done.39.refs_12_ = f32[24,6272]{1,0:T(8,128)S(1)} collective-permute-done((f32[24,6272]{1,0:T(8,128)}, f32[24,6272]{1,0:T(8,128)S(1)}, u32[]{:S(2)}, u32[]{:S(2)}) %collective-permute-start.39) | collective-permute-done | bytes 602144 | tf_op jit(solution)/shard_map/ppermute | solution.py:339
  175.7 11.1 %collective-permute-done.40.refs_13_ = f32[24,6272]{1,0:T(8,128)S(1)} collective-permute-done((f32[24,6272]{1,0:T(8,128)}, f32[24,6272]{1,0:T(8,128)S(1)}, u32[]{:S(2)}, u32[]{:S(2)}) %collective-permute-start.40) | collective-permute-done | bytes 602144 | tf_op jit(solution)/shard_map/ppermute | solution.py:339
  188.2 2.5 collective-permute-start.33
  190.7 39.3 %middle.5 = (f32[24,3584]{1,0:T(8,128)}, f32[24,3584]{1,0:T(8,128)}, f32[24,3584]{1,0:T(8,128)}, f32[24,3584]{1,0:T(8,128)}, f32[24,3584]{1,0:T(8,128)}, /*index...) custom-call(f32[1,24]{1,0:T(1,128)} %get-tuple-element.126.refs_0_, ...), custom_call_target="tpu_custom_call" | custom-call | flops 8455716864 | bytes 9633792 | tf_op jit(solution)/shard_map/middle/pallas_call | solution.py:208
  236.1 12.5 %collective-permute-done.56.refs_20_ = f32[24,896]{1,0:T(8,128)S(1)} collective-permute-done((f32[24,896]{1,0:T(8,128)}, f32[24,896]{1,0:T(8,128)S(1)}, u32[]{:S(2)}, u32[]{:S(2)}) %collective-permute-start.56) | collective-permute-done | bytes 86048 | tf_op jit(solution)/shard_map/ppermute | solution.py:339
  250.5 13.5 %collective-permute-done.49.refs_20_ = f32[24,1792]{1,0:T(8,128)S(1)} collective-permute-done((f32[24,1792]{1,0:T(8,128)}, f32[24,1792]{1,0:T(8,128)S(1)}, u32[]{:S(2)}, u32[]{:S(2)}) %collective-permute-start.49) | collective-permute-done | bytes 172064 | tf_op jit(solution)/shard_map/ppermute | solution.py:339
  264.7 4.9 %collective-permute-done.50.refs_21_ = f32[24,1792]{1,0:T(8,128)S(1)} collective-permute-done((f32[24,1792]{1,0:T(8,128)}, f32[24,1792]{1,0:T(8,128)S(1)}, u32[]{:S(2)}, u32[]{:S(2)}) %collective-permute-start.50) | collective-permute-done | bytes 172064 | tf_op jit(solution)/shard_map/ppermute | solution.py:339
  276.4 11.5 %collective-permute-done.18.refs_7_.refs_8_ = f32[24,6272]{1,0:T(8,128)S(1)} collective-permute-done((f32[24,6272]{1,0:T(8,128)}, f32[24,6272]{1,0:T(8,128)S(1)}, u32[]{:S(2)}, u32[]{:S(2)}) %collective-permute-start.18) | collective-permute-done | bytes 602144 | tf_op jit(solution)/shard_map/ppermute | solution.py:339
  288.0 11.0 %collective-permute-done.19.refs_8_.refs_9_ = f32[24,6272]{1,0:T(8,128)} collective-permute-done((f32[24,6272]{1,0:T(8,128)}, f32[24,6272]{1,0:T(8,128)}, u32[]{:S(2)}, u32[]{:S(2)}) %collective-permute-start.19) | collective-permute-done | bytes 602144 | tf_op jit(solution)/shard_map/ppermute | solution.py:339
  298.9 2.2 collective-permute-start.45
  302.5 2.5 collective-permute-done.42.refs_19_
  308.2 5.8 %collective-permute-done.44.refs_21_ = f32[24,3584]{1,0:T(8,128)} collective-permute-done((f32[24,3584]{1,0:T(8,128)}, f32[24,3584]{1,0:T(8,128)}, u32[]{:S(2)}, u32[]{:S(2)}) %collective-permute-start.44) | collective-permute-done | bytes 344096 | tf_op jit(solution)/shard_map/ppermute | solution.py:339
  315.2 6.5 %collective-permute-done.46.refs_23_ = f32[24,3584]{1,0:T(8,128)} collective-permute-done((f32[24,3584]{1,0:T(8,128)}, f32[24,3584]{1,0:T(8,128)}, u32[]{:S(2)}, u32[]{:S(2)}) %collective-permute-start.46) | collective-permute-done | bytes 344096 | tf_op jit(solution)/shard_map/ppermute | solution.py:339
  322.6 3.9 %collective-permute-done.47.refs_24_ = f32[24,3584]{1,0:T(8,128)} collective-permute-done((f32[24,3584]{1,0:T(8,128)}, f32[24,3584]{1,0:T(8,128)}, u32[]{:S(2)}, u32[]{:S(2)}) %collective-permute-start.47) | collective-permute-done | bytes 344096 | tf_op jit(solution)/shard_map/ppermute | solution.py:339
  326.6 2.8 collective-permute-start.54
  329.5 9.4 %last.3.refs_2_ = f32[6272,448]{1,0:T(8,128)} custom-call(s32[1]{0:T(128)} %bitcast.refs_0_, f32[2,224,224]{2,1,0:T(8,128)} %pad_maximum_fusion.refs_1_, f32[24,6272]{1,0:T(8,128)} %get-tuple-element.101.refs_2_.refs_3_, f32[24,6272]{1,0:T(8,128)} %copy-done.1, f32[24,6272]{1,0:T(8,128)} %copy-done.2, f32[24,6272]{1,0:T(8,128)} %copy-done.3, ...), custom_call_target="tpu_custom_call" | custom-call | flops 2157969408 | bytes 12845056 | tf_op jit(solution)/shard_map/last/pallas_call | solution.py:275
  344.3 5.9 %last.4.refs_2_ = f32[6272,448]{1,0:T(8,128)} custom-call(s32[1]{0:T(128)} %bitcast.refs_0_, f32[2,224,224]{2,1,0:T(8,128)} %pad_maximum_fusion.refs_1_, f32[6272,448]{1,0:T(8,128)} %last.3.refs_2_, f32[24,6272]{1,0:T(8,128)} %get-tuple-element.101.refs_2_.refs_3_, f32[24,6272]{1,0:T(8,128)} %copy-done.1, ...), custom_call_target="tpu_custom_call", output_to_operand_aliasing={{}: (2, {})} | custom-call | flops 1078984704 | bytes 6422528 | tf_op jit(solution)/shard_map/last/pallas_call | solution.py:275
  351.0 4.3 %last.5 = f32[6272,448]{1,0:T(8,128)} custom-call(s32[1]{0:T(128)} %bitcast.refs_0_, f32[2,224,224]{2,1,0:T(8,128)} %pad_maximum_fusion.refs_1_, f32[6272,448]{1,0:T(8,128)} %last.4.refs_2_, f32[24,6272]{1,0:T(8,128)} %get-tuple-element.101.refs_2_.refs_3_, f32[24,6272]{1,0:T(8,128)} %copy-done.1, ...), custom_call_target="tpu_custom_call", output_to_operand_aliasing={{}: (2, {})} | custom-call | flops 539492352 | bytes 3211264 | tf_op jit(solution)/shard_map/last/pallas_call | solution.py:275
  (243 shorter events, 64.9 us)
Async XLA Ops:
  4.5 43.9 %collective-permute-start = (f32[24,2688]{1,0:T(8,128)}, f32[24,2688]{1,0:T(8,128)S(1)}, u32[]{:S(2)}, u32[]{:S(2)}) collective-permute-start(f32[24,2688]{1,0:T(8,128)} %get-tuple-element.87), channel_id=1, source_target_pairs={{0,8},{1,9},{4,12},{5,13},{8,0},{9,1},{12,4},{13,5},{2,10},{3,11},... | collective-permute-start | bytes 774152 | tf_op jit(solution)/shard_map/ppermute | solution.py:339
  7.6 41.7 %collective-permute-start.1 = (f32[24,2688]{1,0:T(8,128)}, f32[24,2688]{1,0:T(8,128)}, u32[]{:S(2)}, u32[]{:S(2)}) collective-permute-start(f32[24,2688]{1,0:T(8,128)} %get-tuple-element.88), channel_id=1, source_target_pairs={{0,1},{1,0},{4,5},{5,4},{8,9},{9,8},{12,13},{13,12},{2,3},{3,2},{6... | collective-permute-start | bytes 774152 | tf_op jit(solution)/shard_map/ppermute | solution.py:339
  57.3 30.1 %collective-permute-start.9 = (f32[24,3584]{1,0:T(8,128)}, f32[24,3584]{1,0:T(8,128)S(1)}, u32[]{:S(2)}, u32[]{:S(2)}) collective-permute-start(f32[24,3584]{1,0:T(8,128)} %get-tuple-element.96), channel_id=1, source_target_pairs={{0,12},{1,13},{4,8},{5,9},{8,4},{9,5},{12,0},{13,1},{2,14},{3,15},... | collective-permute-start | bytes 1032200 | tf_op jit(solution)/shard_map/ppermute | solution.py:339
  61.1 27.8 %collective-permute-start.10 = (f32[24,3584]{1,0:T(8,128)}, f32[24,3584]{1,0:T(8,128)S(1)}, u32[]{:S(2)}, u32[]{:S(2)}) collective-permute-start(f32[24,3584]{1,0:T(8,128)} %get-tuple-element.97), channel_id=1, source_target_pairs={{0,5},{1,4},{4,1},{5,0},{8,13},{9,12},{12,9},{13,8},{2,7},{3,6},{6... | collective-permute-start | bytes 1032200 | tf_op jit(solution)/shard_map/ppermute | solution.py:339
  62.1 27.6 %collective-permute-start.11 = (f32[24,3584]{1,0:T(8,128)S(1)}, f32[24,3584]{1,0:T(8,128)}, u32[]{:S(2)}, u32[]{:S(2)}) collective-permute-start(f32[24,3584]{1,0:T(8,128)S(1)} %copy-done.34), channel_id=1, source_target_pairs={{0,9},{1,8},{4,13},{5,12},{8,1},{9,0},{12,5},{13,4},{2,11},{3,10},... | collective-permute-start | bytes 1032200 | tf_op jit(solution)/shard_map/ppermute | solution.py:339
  87.3 44.5 %collective-permute-start.25 = (f32[8,6272]{1,0:T(8,128)}, f32[8,6272]{1,0:T(8,128)S(1)}, u32[]{:S(2)}, u32[]{:S(2)}) collective-permute-start(f32[8,6272]{1,0:T(8,128)} %get-tuple-element.115), channel_id=1, source_target_pairs={{0,9},{1,8},{4,13},{5,12},{8,1},{9,0},{12,5},{13,4},{2,11},{3,10},... | collective-permute-start | bytes 602120 | tf_op jit(solution)/shard_map/ppermute | solution.py:339
  88.8 43.3 %collective-permute-start.26 = (f32[8,6272]{1,0:T(8,128)}, f32[8,6272]{1,0:T(8,128)S(1)}, u32[]{:S(2)}, u32[]{:S(2)}) collective-permute-start(f32[8,6272]{1,0:T(8,128)} %get-tuple-element.116), channel_id=1, source_target_pairs={{0,13},{1,12},{4,9},{5,8},{8,5},{9,4},{12,1},{13,0},{2,15},{3,14},... | collective-permute-start | bytes 602120 | tf_op jit(solution)/shard_map/ppermute | solution.py:339
  89.7 43.9 %collective-permute-start.27 = (f32[8,6272]{1,0:T(8,128)}, f32[8,6272]{1,0:T(8,128)}, u32[]{:S(2)}, u32[]{:S(2)}) collective-permute-start(f32[8,6272]{1,0:T(8,128)} %get-tuple-element.117), channel_id=1, source_target_pairs={{0,4},{1,5},{4,0},{5,1},{8,12},{9,13},{12,8},{13,9},{2,6},{3,7},{6... | collective-permute-start | bytes 602120 | tf_op jit(solution)/shard_map/ppermute | solution.py:339
  90.5 69.0 %collective-permute-start.35 = (f32[24,6272]{1,0:T(8,128)}, f32[24,6272]{1,0:T(8,128)S(1)}, u32[]{:S(2)}, u32[]{:S(2)}) collective-permute-start(f32[24,6272]{1,0:T(8,128)} %get-tuple-element.128), channel_id=1, source_target_pairs={{0,8},{1,9},{4,12},{5,13},{8,0},{9,1},{12,4},{13,5},{2,10},{3,11},... | collective-permute-start | bytes 1806344 | tf_op jit(solution)/shard_map/ppermute | solution.py:339
  90.8 68.9 %collective-permute-start.36 = (f32[24,6272]{1,0:T(8,128)}, f32[24,6272]{1,0:T(8,128)S(1)}, u32[]{:S(2)}, u32[]{:S(2)}) collective-permute-start(f32[24,6272]{1,0:T(8,128)} %get-tuple-element.129), channel_id=1, source_target_pairs={{0,1},{1,0},{4,5},{5,4},{8,9},{9,8},{12,13},{13,12},{2,3},{3,2},{6... | collective-permute-start | bytes 1806344 | tf_op jit(solution)/shard_map/ppermute | solution.py:339
  131.8 30.1 %collective-permute-start.37 = (f32[24,6272]{1,0:T(8,128)}, f32[24,6272]{1,0:T(8,128)}, u32[]{:S(2)}, u32[]{:S(2)}) collective-permute-start(f32[24,6272]{1,0:T(8,128)} %get-tuple-element.130), channel_id=1, source_target_pairs={{0,12},{1,13},{4,8},{5,9},{8,4},{9,5},{12,0},{13,1},{2,14},{3,15},... | collective-permute-start | bytes 1806344 | tf_op jit(solution)/shard_map/ppermute | solution.py:339
  132.2 30.6 %collective-permute-start.38 = (f32[24,6272]{1,0:T(8,128)}, f32[24,6272]{1,0:T(8,128)}, u32[]{:S(2)}, u32[]{:S(2)}) collective-permute-start(f32[24,6272]{1,0:T(8,128)} %get-tuple-element.131), channel_id=1, source_target_pairs={{0,5},{1,4},{4,1},{5,0},{8,13},{9,12},{12,9},{13,8},{2,7},{3,6},{6... | collective-permute-start | bytes 1806344 | tf_op jit(solution)/shard_map/ppermute | solution.py:339
  159.6 27.2 %collective-permute-start.40 = (f32[24,6272]{1,0:T(8,128)}, f32[24,6272]{1,0:T(8,128)S(1)}, u32[]{:S(2)}, u32[]{:S(2)}) collective-permute-start(f32[24,6272]{1,0:T(8,128)} %get-tuple-element.133), channel_id=1, source_target_pairs={{0,13},{1,12},{4,9},{5,8},{8,5},{9,4},{12,1},{13,0},{2,15},{3,14},... | collective-permute-start | bytes 1806344 | tf_op jit(solution)/shard_map/ppermute | solution.py:339
  159.7 28.5 %collective-permute-start.41 = (f32[24,6272]{1,0:T(8,128)S(1)}, f32[24,6272]{1,0:T(8,128)S(1)}, u32[]{:S(2)}, u32[]{:S(2)}) collective-permute-start(f32[24,6272]{1,0:T(8,128)S(1)} %copy-done.27), channel_id=1, source_target_pairs={{0,4},{1,5},{4,0},{5,1},{8,12},{9,13},{12,8},{13,9},{2,6},{3,7},{6... | collective-permute-start | bytes 1806344 | tf_op jit(solution)/shard_map/ppermute | solution.py:339
  161.9 68.1 %collective-permute-start.29 = (f32[8,6272]{1,0:T(8,128)}, f32[8,6272]{1,0:T(8,128)S(1)}, u32[]{:S(2)}, u32[]{:S(2)}) collective-permute-start(f32[8,6272]{1,0:T(8,128)} %get-tuple-element.120), channel_id=1, source_target_pairs={{0,1},{1,0},{4,5},{5,4},{8,9},{9,8},{12,13},{13,12},{2,3},{3,2},{6... | collective-permute-start | bytes 602120 | tf_op jit(solution)/shard_map/ppermute | solution.py:339
  162.8 68.1 %collective-permute-start.30 = (f32[8,6272]{1,0:T(8,128)}, f32[8,6272]{1,0:T(8,128)S(1)}, u32[]{:S(2)}, u32[]{:S(2)}) collective-permute-start(f32[8,6272]{1,0:T(8,128)} %get-tuple-element.121), channel_id=1, source_target_pairs={{0,12},{1,13},{4,8},{5,9},{8,4},{9,5},{12,0},{13,1},{2,14},{3,15},... | collective-permute-start | bytes 602120 | tf_op jit(solution)/shard_map/ppermute | solution.py:339
  175.7 57.2 %collective-permute-start.31 = (f32[8,6272]{1,0:T(8,128)}, f32[8,6272]{1,0:T(8,128)S(1)}, u32[]{:S(2)}, u32[]{:S(2)}) collective-permute-start(f32[8,6272]{1,0:T(8,128)} %get-tuple-element.122), channel_id=1, source_target_pairs={{0,5},{1,4},{4,1},{5,0},{8,13},{9,12},{12,9},{13,8},{2,7},{3,6},{6... | collective-permute-start | bytes 602120 | tf_op jit(solution)/shard_map/ppermute | solution.py:339
  186.8 46.1 %collective-permute-start.32 = (f32[8,6272]{1,0:T(8,128)}, f32[8,6272]{1,0:T(8,128)S(1)}, u32[]{:S(2)}, u32[]{:S(2)}) collective-permute-start(f32[8,6272]{1,0:T(8,128)} %get-tuple-element.123), channel_id=1, source_target_pairs={{0,9},{1,8},{4,13},{5,12},{8,1},{9,0},{12,5},{13,4},{2,11},{3,10},... | collective-permute-start | bytes 602120 | tf_op jit(solution)/shard_map/ppermute | solution.py:339
  188.2 45.5 %collective-permute-start.33 = (f32[8,6272]{1,0:T(8,128)}, f32[8,6272]{1,0:T(8,128)S(1)}, u32[]{:S(2)}, u32[]{:S(2)}) collective-permute-start(f32[8,6272]{1,0:T(8,128)} %get-tuple-element.124), channel_id=1, source_target_pairs={{0,13},{1,12},{4,9},{5,8},{8,5},{9,4},{12,1},{13,0},{2,15},{3,14},... | collective-permute-start | bytes 602120 | tf_op jit(solution)/shard_map/ppermute | solution.py:339
  230.0 41.7 %collective-permute-start.14 = (f32[24,6272]{1,0:T(8,128)}, f32[24,6272]{1,0:T(8,128)S(1)}, u32[]{:S(2)}, u32[]{:S(2)}) collective-permute-start(f32[24,6272]{1,0:T(8,128)} %get-tuple-element.102), channel_id=1, source_target_pairs={{0,8},{1,9},{4,12},{5,13},{8,0},{9,1},{12,4},{13,5},{2,10},{3,11},... | collective-permute-start | bytes 1806344 | tf_op jit(solution)/shard_map/ppermute | solution.py:339
  231.6 40.1 %collective-permute-start.15 = (f32[24,6272]{1,0:T(8,128)}, f32[24,6272]{1,0:T(8,128)S(1)}, u32[]{:S(2)}, u32[]{:S(2)}) collective-permute-start(f32[24,6272]{1,0:T(8,128)} %get-tuple-element.103), channel_id=1, source_target_pairs={{0,1},{1,0},{4,5},{5,4},{8,9},{9,8},{12,13},{13,12},{2,3},{3,2},{6... | collective-permute-start | bytes 1806344 | tf_op jit(solution)/shard_map/ppermute | solution.py:339
  235.7 37.6 %collective-permute-start.16 = (f32[24,6272]{1,0:T(8,128)}, f32[24,6272]{1,0:T(8,128)S(1)}, u32[]{:S(2)}, u32[]{:S(2)}) collective-permute-start(f32[24,6272]{1,0:T(8,128)} %get-tuple-element.104), channel_id=1, source_target_pairs={{0,12},{1,13},{4,8},{5,9},{8,4},{9,5},{12,0},{13,1},{2,14},{3,15},... | collective-permute-start | bytes 1806344 | tf_op jit(solution)/shard_map/ppermute | solution.py:339
  248.6 25.6 %collective-permute-start.17 = (f32[24,6272]{1,0:T(8,128)}, f32[24,6272]{1,0:T(8,128)S(1)}, u32[]{:S(2)}, u32[]{:S(2)}) collective-permute-start(f32[24,6272]{1,0:T(8,128)} %get-tuple-element.105), channel_id=1, source_target_pairs={{0,5},{1,4},{4,1},{5,0},{8,13},{9,12},{12,9},{13,8},{2,7},{3,6},{6... | collective-permute-start | bytes 1806344 | tf_op jit(solution)/shard_map/ppermute | solution.py:339
  271.7 27.2 %collective-permute-start.19 = (f32[24,6272]{1,0:T(8,128)}, f32[24,6272]{1,0:T(8,128)}, u32[]{:S(2)}, u32[]{:S(2)}) collective-permute-start(f32[24,6272]{1,0:T(8,128)} %get-tuple-element.107), channel_id=1, source_target_pairs={{0,13},{1,12},{4,9},{5,8},{8,5},{9,4},{12,1},{13,0},{2,15},{3,14},... | collective-permute-start | bytes 1806344 | tf_op jit(solution)/shard_map/ppermute | solution.py:339
  271.7 29.4 %collective-permute-start.20 = (f32[24,6272]{1,0:T(8,128)}, f32[24,6272]{1,0:T(8,128)}, u32[]{:S(2)}, u32[]{:S(2)}) collective-permute-start(f32[24,6272]{1,0:T(8,128)} %get-tuple-element.108), channel_id=1, source_target_pairs={{0,4},{1,5},{4,0},{5,1},{8,12},{9,13},{12,8},{13,9},{2,6},{3,7},{6... | collective-permute-start | bytes 1806344 | tf_op jit(solution)/shard_map/ppermute | solution.py:339
  273.4 31.7 %collective-permute-start.42 = (f32[24,3584]{1,0:T(8,128)}, f32[24,3584]{1,0:T(8,128)S(1)}, u32[]{:S(2)}, u32[]{:S(2)}) collective-permute-start(f32[24,3584]{1,0:T(8,128)} %get-tuple-element.136), channel_id=1, source_target_pairs={{0,8},{1,9},{4,12},{5,13},{8,0},{9,1},{12,4},{13,5},{2,10},{3,11},... | collective-permute-start | bytes 1032200 | tf_op jit(solution)/shard_map/ppermute | solution.py:339
  274.2 31.8 %collective-permute-start.43 = (f32[24,3584]{1,0:T(8,128)}, f32[24,3584]{1,0:T(8,128)S(1)}, u32[]{:S(2)}, u32[]{:S(2)}) collective-permute-start(f32[24,3584]{1,0:T(8,128)} %get-tuple-element.137), channel_id=1, source_target_pairs={{0,1},{1,0},{4,5},{5,4},{8,9},{9,8},{12,13},{13,12},{2,3},{3,2},{6... | collective-permute-start | bytes 1032200 | tf_op jit(solution)/shard_map/ppermute | solution.py:339
  288.0 26.0 %collective-permute-start.44 = (f32[24,3584]{1,0:T(8,128)}, f32[24,3584]{1,0:T(8,128)}, u32[]{:S(2)}, u32[]{:S(2)}) collective-permute-start(f32[24,3584]{1,0:T(8,128)} %get-tuple-element.138), channel_id=1, source_target_pairs={{0,12},{1,13},{4,8},{5,9},{8,4},{9,5},{12,0},{13,1},{2,14},{3,15},... | collective-permute-start | bytes 1032200 | tf_op jit(solution)/shard_map/ppermute | solution.py:339
  305.0 21.6 %collective-permute-start.47 = (f32[24,3584]{1,0:T(8,128)}, f32[24,3584]{1,0:T(8,128)}, u32[]{:S(2)}, u32[]{:S(2)}) collective-permute-start(f32[24,3584]{1,0:T(8,128)} %get-tuple-element.141), channel_id=1, source_target_pairs={{0,13},{1,12},{4,9},{5,8},{8,5},{9,4},{12,1},{13,0},{2,15},{3,14},... | collective-permute-start | bytes 1032200 | tf_op jit(solution)/shard_map/ppermute | solution.py:339
  305.9 23.5 %collective-permute-start.48 = (f32[24,3584]{1,0:T(8,128)}, f32[24,3584]{1,0:T(8,128)}, u32[]{:S(2)}, u32[]{:S(2)}) collective-permute-start(f32[24,3584]{1,0:T(8,128)} %get-tuple-element.142), channel_id=1, source_target_pairs={{0,4},{1,5},{4,0},{5,1},{8,12},{9,13},{12,8},{13,9},{2,6},{3,7},{6... | collective-permute-start | bytes 1032200 | tf_op jit(solution)/shard_map/ppermute | solution.py:339
  314.0 24.9 %collective-permute-start.51 = (f32[24,1792]{1,0:T(8,128)}, f32[24,1792]{1,0:T(8,128)}, u32[]{:S(2)}, u32[]{:S(2)}) collective-permute-start(f32[24,1792]{1,0:T(8,128)} %get-tuple-element.146), channel_id=1, source_target_pairs={{0,12},{1,13},{4,8},{5,9},{8,4},{9,5},{12,0},{13,1},{2,14},{3,15},... | collective-permute-start | bytes 516104 | tf_op jit(solution)/shard_map/ppermute | solution.py:339
  314.1 26.0 %collective-permute-start.52 = (f32[24,1792]{1,0:T(8,128)}, f32[24,1792]{1,0:T(8,128)}, u32[]{:S(2)}, u32[]{:S(2)}) collective-permute-start(f32[24,1792]{1,0:T(8,128)} %get-tuple-element.147), channel_id=1, source_target_pairs={{0,5},{1,4},{4,1},{5,0},{8,13},{9,12},{12,9},{13,8},{2,7},{3,6},{6... | collective-permute-start | bytes 516104 | tf_op jit(solution)/shard_map/ppermute | solution.py:339
  (75 other events, 1511.4 us)
